TPU v7x, 512 devices: a whole 4x4x16 slice. The times are simulated.
512 devices in a mesh: dp: 64 (over z, y_lo, core), mp: 8 (over x, y_hi).
Axes of the slice: x: 4, y: 4 (y_hi: 2, y_lo: 2; y = y_hi * 2 + y_lo), z: 16, core: 2. Of those that a mesh axis runs over, the one named last changes fastest.
Arguments:
- picture_tower_vectors: bfloat16 [12288, 1152], P('dp'), may hold values from -6 to 6
- caption_tower_vectors: bfloat16 [12288, 1152], P('dp', 'mp'), may hold values from -6 to 6
- picture_standardize_factor: float32 [1152], replicated, may hold values from 0.1 to 1.9
- picture_entry_matrix: bfloat16 [1152, 4304], P(None, 'mp'), may hold values from -0.1875 to 0.1875
- picture_exit_matrix: bfloat16 [4304, 1152], P('mp'), may hold values from -0.09375 to 0.09375
- caption_mapping_matrix: bfloat16 [1152, 1152], P('mp'), may hold values from -1 to 1
- energy_multiplier: float32 [], replicated, may hold values from 4 to 16
- energy_offset_term: float32 [], replicated, may hold values from -2 to -0.5
Outputs:
- grad_image: float32 [12288, 1152], P('dp', 'mp')
- grad_text: float32 [12288, 1152], P('dp', 'mp')
All inputs are finite; a program needn't handle non-finite values.
Results may differ from a plain program's by a relative error of at most 0.0046.
Values may be sent and summed in bfloat16 or wider, within the bound.
No kernel may reach another device: no remote copies, remote signals or barrier semaphores. Data moves between devices by JAX's collectives and lax.ppermute only.
A program may use at most 64 MiB of HBM per device.

v0:
```python
import jax
import jax.numpy as jnp
from jax import lax
from jax.sharding import Mesh
from jax.sharding import PartitionSpec as P

DP = ("dp_0", "dp_1", "dp_2")


def cut_along(array, dim, peers):
    lengths = array.shape
    parts = array.reshape(*lengths[:dim], peers, lengths[dim] // peers, *lengths[dim + 1 :])
    return jnp.moveaxis(parts, dim, 0)


def summed_on_arrival(array, axis, dim):
    peers = lax.axis_size(axis)
    parts = lax.all_to_all(cut_along(array, dim, peers), axis, 0, 0, tiled=True)
    return jnp.sum(parts.astype(jnp.float32), axis=0)


def in_order(parts, dim):
    lengths = list(parts.shape[1:])
    lengths[dim] *= parts.shape[0]
    return jnp.moveaxis(parts, 0, dim).reshape(lengths)


def stacked_from(array, axes, order):
    parts = array[None]
    for k in order:
        parts = lax.all_gather(parts, axes[k], axis=0, tiled=True)
    block = [lax.axis_size(axes[k]) for k in reversed(order)]
    parts = parts.reshape(*block, *array.shape)
    turned = sorted(range(len(order)), key=lambda place: order[len(order) - 1 - place])
    return parts.transpose(*turned, *range(len(order), parts.ndim)).reshape(-1, *array.shape)


def whole_of(array, axes, order, dim):
    return in_order(stacked_from(array, axes, order), dim)


def sum_at_owner(array, axis, dim):
    parts = cut_along(array, dim, lax.axis_size(axis))
    arrived = lax.all_to_all(parts, axis, split_axis=0, concat_axis=0, tiled=True)
    return arrived.sum(axis=0)


def sent_to_all(array, axis):
    copies = jnp.broadcast_to(array, (lax.axis_size(axis), *array.shape))
    return lax.all_to_all(copies, axis, split_axis=0, concat_axis=0, tiled=True)


def collect(array, axis, dim):
    return in_order(sent_to_all(array, axis), dim)


def of_everyone(array, axis):
    return sent_to_all(array, axis).sum(axis=0)


def together(arrays, axis):
    ends = [0]
    for a in arrays:
        ends.append(ends[-1] + a.size)
    so_far = of_everyone(jnp.concatenate([a.ravel() for a in arrays]), axis)
    return tuple((so_far[b:e].reshape(a.shape) for a, b, e in zip(arrays, ends, ends[1:])))


def gelu_tanh(values):
    return jax.nn.gelu(values, approximate=True)


def norm_back(upstream, unit_rows, inverse):
    unit_float = unit_rows.astype(jnp.float32)
    along = jnp.sum(unit_float * upstream, axis=-1, keepdims=True)
    return inverse * (upstream - unit_float * along)


def per_device(
    picture_tower_vectors,
    caption_tower_vectors,
    picture_standardize_factor,
    picture_entry_matrix,
    picture_exit_matrix,
    caption_mapping_matrix,
    energy_multiplier,
    energy_offset_term,
):
    rows_here = picture_tower_vectors.shape[0]
    width = picture_tower_vectors.shape[1]
    head_count = lax.axis_size("mp")
    head_pos = lax.axis_index("mp")
    cycle_size = lax.axis_size(DP)
    cycle_pos = lax.axis_index(DP)
    share = rows_here // head_count
    cols_here = caption_tower_vectors.shape[1]
    image_float = picture_tower_vectors.astype(jnp.float32)
    mean_row = jnp.mean(image_float, axis=-1, keepdims=True)
    variance = jnp.mean((image_float - mean_row) ** 2, axis=-1, keepdims=True)
    inv_std = lax.rsqrt(variance + 1e-06)
    centred = (image_float - mean_row) * inv_std
    normed = (centred * picture_standardize_factor).astype(jnp.bfloat16)
    preact = jnp.dot(normed, picture_entry_matrix, preferred_element_type=jnp.float32)
    hidden = gelu_tanh(preact).astype(jnp.bfloat16)
    partial_out = jnp.dot(hidden, picture_exit_matrix, preferred_element_type=jnp.float32)
    image_out = image_float + lax.psum(partial_out, "mp")
    inv_image = lax.rsqrt(jnp.sum(image_out * image_out, axis=-1, keepdims=True) + 1e-06)
    unit_image = (image_out * inv_image).astype(jnp.bfloat16)
    text_out = summed_on_arrival(
        jnp.dot(
            caption_tower_vectors, caption_mapping_matrix, preferred_element_type=jnp.float32
        ).astype(jnp.bfloat16),
        "mp",
        0,
    )
    inv_text = lax.rsqrt(jnp.sum(text_out * text_out, axis=-1, keepdims=True) + 1e-06)
    unit_text = (text_out * inv_text).astype(jnp.bfloat16)
    image_ids = cycle_pos * rows_here + jnp.arange(rows_here, dtype=jnp.int32)
    piece = whole_of(unit_text, DP, (1, 0, 2), 0)
    count = piece.shape[0]
    whole_pos = jnp.arange(count, dtype=jnp.int32)
    text_ids = whole_pos // share * rows_here + head_pos * share + whole_pos % share
    cosine_matrix = lax.dot_general(
        piece, unit_image, (((1,), (1,)), ((), ())), preferred_element_type=jnp.float32
    )
    couple_energies = energy_multiplier * cosine_matrix + energy_offset_term
    match_polarity = jnp.where(text_ids[:, None] == image_ids[None, :], 1.0, -1.0).astype(
        jnp.float32
    )
    polarity_scaled_energies = (
        energy_multiplier * -match_polarity * jax.nn.sigmoid(-match_polarity * couple_energies)
    ).astype(jnp.bfloat16)
    image_add = lax.dot_general(
        polarity_scaled_energies,
        piece,
        (((0,), (0,)), ((), ())),
        preferred_element_type=jnp.float32,
    )
    text_add = jnp.dot(polarity_scaled_energies, unit_image, preferred_element_type=jnp.float32)
    image_add, text_add = (image_add, text_add)
    text_store = text_add
    image_dir, text_store = (image_add, text_store)
    returned = lax.all_to_all(
        text_store.astype(jnp.bfloat16), DP, split_axis=0, concat_axis=0, tiled=True
    ).astype(text_store.dtype)
    text_dir = jnp.sum(returned.reshape(cycle_size, share, width), axis=0)
    image_share = sum_at_owner(image_dir, "mp", 0)
    first_row = head_pos * share
    unit_share = lax.dynamic_slice_in_dim(unit_image, first_row, share, 0)
    inv_share = lax.dynamic_slice_in_dim(inv_image, first_row, share, 0)
    grad_share = norm_back(image_share, unit_share, inv_share)
    grad_out = collect(grad_share, "mp", 0)
    grad_out_b = grad_out.astype(jnp.bfloat16)
    grad_hidden = lax.dot_general(
        grad_out_b,
        picture_exit_matrix,
        (((1,), (1,)), ((), ())),
        preferred_element_type=jnp.float32,
    )
    unused, pull_back = jax.vjp(gelu_tanh, preact)
    grad_pre = pull_back(grad_hidden)[0].astype(jnp.bfloat16)
    partial_normed = lax.dot_general(
        grad_pre, picture_entry_matrix, (((1,), (1,)), ((), ())), preferred_element_type=jnp.float32
    )
    grad_normed = sum_at_owner(partial_normed, "mp", 1)
    first_col = head_pos * cols_here
    gain_here = lax.dynamic_slice_in_dim(picture_standardize_factor, first_col, cols_here, 0)
    centred_here = lax.dynamic_slice_in_dim(centred, first_col, cols_here, 1)
    grad_out_here = lax.dynamic_slice_in_dim(grad_out, first_col, cols_here, 1)
    scaled = grad_normed * gain_here
    sum_one, sum_two = together(
        (jnp.sum(scaled, axis=-1), jnp.sum(scaled * centred_here, axis=-1)), "mp"
    )
    mean_one = (sum_one / width)[:, None]
    mean_two = (sum_two / width)[:, None]
    grad_image = grad_out_here + inv_std * (scaled - mean_one - centred_here * mean_two)
    grad_text_out = norm_back(text_dir, unit_text, inv_text).astype(jnp.bfloat16)
    grad_text = lax.dot_general(
        collect(grad_text_out, "mp", 0),
        caption_mapping_matrix,
        (((1,), (1,)), ((), ())),
        preferred_element_type=jnp.float32,
    )
    return (grad_image, grad_text)


def solution(mesh):
    split = Mesh(mesh.devices.reshape(16, 2, 2, mesh.shape["mp"]), ("dp_0", "dp_1", "dp_2", "mp"))
    in_specs = (
        P(DP, None),
        P(DP, "mp"),
        P(),
        P(None, "mp"),
        P("mp", None),
        P("mp", None),
        P(),
        P(),
    )
    out_specs = (P(DP, "mp"), P(DP, "mp"))
    return jax.shard_map(
        per_device, mesh=split, in_specs=in_specs, out_specs=out_specs, check_vma=False
    )
```

profile of v0, /device:TPU:8, one launch (start us, length us, event | category | flops | bytes accessed | tf_op | source)
XLA Modules:
  0.0 417.5 jit_solution(5761427556059178533)
XLA Ops:
  8.1 1.4 convolution_convert_fusion.1
  9.5 16.4 %all_to_all.40 = bf16[8,24,1152]{2,1,0:T(8,128)(2,1)S(1)} all-to-all(bf16[8,24,1152]{2,1,0:T(8,128)(2,1)S(1)} %bitcast.50), channel_id=1, replica_groups=mesh['dp_0'=16,'dp_1'=2,'dp_2'=2,'mp'=8] {'mp'}, dimensions={0} | all-to-all | bytes 884736 | tf_op jit(solution)/shard_map/all_to_all | solution.py:18
  26.2 4.9 %all_gather.9 = bf16[2,24,1152]{2,1,0:T(8,128)(2,1)} all-gather(bf16[1,24,1152]{2,1,0:T(8,128)(2,1)S(1)} %fusion.50), channel_id=1, replica_groups=mesh['dp_0'=16,'dp_1'=2,'dp_2'=2,'mp'=8] {'dp_1'}, dimensions={0}, use_global_device_ids=true | all-gather | bytes 165888 | tf_op jit(solution)/shard_map/all_gather | solution.py:31
  31.7 2.0 fusion.22
  33.7 1.5 fusion.32
  35.2 69.5 %all-gather.3.cloned.1.call-done = bf16[32,24,1152]{2,1,0:T(8,128)(2,1)} async-done(((bf16[2,24,1152]{2,1,0:T(8,128)(2,1)}), bf16[32,24,1152]{2,1,0:T(8,128)(2,1)}) %all-gather.3.cloned.1.call-update) | async-done | bytes 1769488 | tf_op jit(solution)/shard_map/all_gather | solution.py:31
  106.1 33.0 %all-reduce.2.cloned.1.call-done = f32[192,1152]{1,0:T(8,128)} async-done(((f32[192,1152]{1,0:T(8,128)}), f32[192,1152]{1,0:T(8,128)}) %all-reduce.2.cloned.1.call-update) | async-done | bytes 884752 | tf_op jit(solution)/shard_map/psum | solution.py:106
  139.1 1.5 multiply_reduce_fusion
  140.9 2.4 copy.22
  143.4 2.5 fusion.6
  145.9 1.9 fusion.74
  147.8 3.8 all-to-all-start.1
  151.6 11.3 %all-to-all-done.1 = f32[8,24,1152]{2,1,0:T(8,128)S(1)} async-done(((f32[8,24,1152]{2,1,0:T(8,128)}), f32[8,24,1152]{2,1,0:T(8,128)S(1)}, u32[]{:S(2)}, u32[]{:S(2)}) %all-to-all-start.1) | async-done | bytes 884768 | tf_op jit(solution)/shard_map/all_to_all | solution.py:44
  162.9 0.9 fusion.43
  163.9 0.9 fusion.45
  164.9 15.6 %all_to_all.41 = f32[8,24,1152]{2,1,0:T(8,128)S(1)} all-to-all(f32[8,24,1152]{2,1,0:T(8,128)S(1)} %broadcast_in_dim.36), channel_id=1, replica_groups=mesh['dp_0'=16,'dp_1'=2,'dp_2'=2,'mp'=8] {'mp'}, dimensions={0} | all-to-all | bytes 1769472 | tf_op jit(solution)/shard_map/all_to_all | solution.py:50
  180.5 4.1 fusion.28
  184.6 3.6 all-to-all-start.3
  188.3 12.4 %all-to-all-done.3 = f32[8,192,144]{1,2,0:T(8,128)S(1)} async-done(((f32[8,192,144]{1,2,0:T(8,128)}), f32[8,192,144]{1,2,0:T(8,128)S(1)}, u32[]{:S(2)}, u32[]{:S(2)}) %all-to-all-start.3) | async-done | bytes 884768 | tf_op jit(solution)/shard_map/all_to_all | solution.py:44
  201.4 1.0 copy.24
  203.3 4.0 all-to-all-start.4
  207.3 4.7 %convolution_convert_fusion = bf16[1536,1152]{1,0:T(8,128)(2,1)} fusion(bf16[192,1152]{1,0:T(8,128)(2,1)} %copy-done.5, f32[1536,192]{0,1:T(8,128)} %get-tuple-element.19, s32[1536]{0:T(1024)S(1)} %fusion.59, f32[]{:T(128)S(6)} %copy.32, s32[192]{0:T(256)S(1)} %iota_add_fusion), kind=kOutput, calls=%fused_computation | convolution fusion | flops 684195840 | bytes 5167876 | tf_op jit(solution)/shard_map/dot_general | solution.py:139
  212.0 2.9 all-to-all-done.4
  215.0 14.4 %all-to-all-start.5 = ((bf16[64,24,1152]{2,1,0:T(8,128)(2,1)}), bf16[64,24,1152]{2,1,0:T(8,128)(2,1)}, u32[]{:S(2)}, u32[]{:S(2)}) async-start(bf16[64,24,1152]{2,1,0:T(8,128)(2,1)} %bitcast.48), calls=%async_computation.5 | async-start | bytes 7077888 | tf_op jit(solution)/shard_map/all_to_all | solution.py:143
  229.4 162.7 %all-to-all-done.5 = bf16[64,24,1152]{2,1,0:T(8,128)(2,1)} async-done(((bf16[64,24,1152]{2,1,0:T(8,128)(2,1)}), bf16[64,24,1152]{2,1,0:T(8,128)(2,1)}, u32[]{:S(2)}, u32[]{:S(2)}) %all-to-all-start.5) | async-done | bytes 3538976 | tf_op jit(solution)/shard_map/all_to_all | solution.py:143
  392.1 2.5 convert_reduce_fusion
  394.9 0.8 broadcast_in_dim.40
  395.7 4.3 %all-to-all-start.6 = ((bf16[8,24,1152]{2,1,0:T(8,128)(2,1)}), bf16[8,24,1152]{2,1,0:T(8,128)(2,1)S(1)}, u32[]{:S(2)}, u32[]{:S(2)}) async-start(bf16[8,24,1152]{2,1,0:T(8,128)(2,1)} %broadcast_in_dim.40), calls=%async_computation.6 | async-start | bytes 884736 | tf_op jit(solution)/shard_map/all_to_all | solution.py:50
  400.0 1.2 multiply_add_fusion
  401.2 0.8 copy.26
  402.0 7.1 %all-to-all-done.6 = bf16[8,24,1152]{2,1,0:T(8,128)(2,1)S(1)} async-done(((bf16[8,24,1152]{2,1,0:T(8,128)(2,1)}), bf16[8,24,1152]{2,1,0:T(8,128)(2,1)S(1)}, u32[]{:S(2)}, u32[]{:S(2)}) %all-to-all-start.6) | async-done | bytes 442400 | tf_op jit(solution)/shard_map/all_to_all | solution.py:50
  409.1 1.0 fusion.75
  (47 shorter events, 3.6 us)
Async XLA Ops:
  8.0 25.7 %copy-start = (bf16[538,1152]{1,0:T(8,128)(2,1)S(1)}, bf16[538,1152]{1,0:T(8,128)(2,1)}, u32[]{:S(2)}) copy-start(bf16[538,1152]{1,0:T(8,128)(2,1)} %param.12) | copy-start | bytes 3718660
  8.0 96.7 %all-gather.3.cloned.1.call-start = ((), (), s32[]{:S(2)}) async-start(), calls=%async_computation.8 | async-start | bytes 1880064 | tf_op jit(solution)/shard_map/all_gather | solution.py:31
  9.5 21.7 %copy-start.1 = (bf16[192,1152]{1,0:T(8,128)(2,1)S(1)}, bf16[192,1152]{1,0:T(8,128)(2,1)}, u32[]{:S(2)}) copy-start(bf16[192,1152]{1,0:T(8,128)(2,1)} %param.8) | copy-start | bytes 1327108
  25.9 5.7 %copy-start.7 = (f32[1152]{0:T(1024)S(1)}, f32[1152]{0:T(1024)}, u32[]{:S(2)}) copy-start(f32[1152]{0:T(1024)} %param.10) | copy-start | bytes 13828
  31.2 107.9 %all-reduce.2.cloned.1.call-start = ((), (), s32[]{:S(2)}) async-start(), calls=%async_computation.7 | async-start | bytes 1769472 | tf_op jit(solution)/shard_map/psum | solution.py:106
  33.7 1.5 copy-start.6
  35.2 105.7 %all-gather.5.cloned.1.call-start = ((), (), s32[]{:S(2)}) async-start(), calls=%async_computation.9 | async-start | bytes 5308416 | tf_op jit(solution)/shard_map/all_gather | solution.py:31
  139.1 1.5 copy-start.2
  140.9 2.5 copy-start.5
  147.8 15.1 %all-to-all-start.1 = ((f32[8,24,1152]{2,1,0:T(8,128)}), f32[8,24,1152]{2,1,0:T(8,128)S(1)}, u32[]{:S(2)}, u32[]{:S(2)}) async-start(f32[8,24,1152]{2,1,0:T(8,128)} %fusion.74), calls=%async_computation.1 | async-start | bytes 1769472 | tf_op jit(solution)/shard_map/all_to_all | solution.py:44
  180.4 4.2 copy-start.4
  184.6 16.0 %all-to-all-start.3 = ((f32[8,192,144]{1,2,0:T(8,128)}), f32[8,192,144]{1,2,0:T(8,128)S(1)}, u32[]{:S(2)}, u32[]{:S(2)}) async-start(f32[8,192,144]{1,2,0:T(8,128)} %bitcast.53), calls=%async_computation.3 | async-start | bytes 2359296 | tf_op jit(solution)/shard_map/all_to_all | solution.py:44
  203.3 11.7 %all-to-all-start.4 = ((f32[8,1,384]{2,1,0:T(1,128)}), f32[8,1,384]{2,1,0:T(1,128)S(1)}, u32[]{:S(2)}, u32[]{:S(2)}) async-start(f32[8,1,384]{2,1,0:T(1,128)} %broadcast_in_dim.37), calls=%async_computation.4 | async-start | bytes 24576 | tf_op jit(solution)/shard_map/all_to_all | solution.py:50
  215.0 177.1 %all-to-all-start.5 = ((bf16[64,24,1152]{2,1,0:T(8,128)(2,1)}), bf16[64,24,1152]{2,1,0:T(8,128)(2,1)}, u32[]{:S(2)}, u32[]{:S(2)}) async-start(bf16[64,24,1152]{2,1,0:T(8,128)(2,1)} %bitcast.48), calls=%async_computation.5 | async-start | bytes 7077888 | tf_op jit(solution)/shard_map/all_to_all | solution.py:143
  394.9 14.2 %copy-start.3 = (bf16[144,1152]{1,0:T(8,128)(2,1)S(1)}, bf16[144,1152]{1,0:T(8,128)(2,1)}, u32[]{:S(2)}) copy-start(bf16[144,1152]{1,0:T(8,128)(2,1)} %param.13) | copy-start | bytes 995332
  395.7 13.4 %all-to-all-start.6 = ((bf16[8,24,1152]{2,1,0:T(8,128)(2,1)}), bf16[8,24,1152]{2,1,0:T(8,128)(2,1)S(1)}, u32[]{:S(2)}, u32[]{:S(2)}) async-start(bf16[8,24,1152]{2,1,0:T(8,128)(2,1)} %broadcast_in_dim.40), calls=%async_computation.6 | async-start | bytes 884736 | tf_op jit(solution)/shard_map/all_to_all | solution.py:50
Sparse Core Ops, SparseCore 0:
  31.3 73.3 all-gather.2
  106.8 20.0 all-gather.4
Sparse Core Ops, SparseCore 1:
  35.3 103.8 all-reduce.1
where the time goes:
time: 419 us; the launch traced here: 418 us
  waiting for transfers between devices  299 us (71%)
  blocking collectives  36.9 us (9%)
  starting transfers between devices  30.1 us (7%)
  matrix products  19.2 us (5%)
  between operations  17 us (4%)
  other arithmetic  9.52 us (2%)
  local copies, waits for them, and re-layouts  5.88 us (1%)
    all_to_all x1, waiting for transfers between devices, per_device(): lax.all_to_all(text_store.astype(jnp.bfloat16), DP, split_axis=0, concat_...  163 us
    all_gather x2, waiting for transfers between devices, stacked_from(): parts = lax.all_gather(parts, axes[k], axis=0, tiled=True)  69.5 us
    psum x1, waiting for transfers between devices, per_device(): image_out = image_float + lax.psum(partial_out, 'mp')  33 us
    all_to_all x2, waiting for transfers between devices, sum_at_owner(): lax.all_to_all(parts, axis, split_axis=0, concat_axis=0, tiled=True)  23.6 us
    all_to_all x1, blocking collectives, summed_on_arrival(): parts = lax.all_to_all(cut_along(array, dim, peers), axis, 0, 0, tiled=True)  16.4 us
    all_to_all x1, blocking collectives, sent_to_all(): return lax.all_to_all(copies, axis, split_axis=0, concat_axis=0, tiled=True)  15.6 us
    all_to_all x1, starting transfers between devices, per_device(): lax.all_to_all(text_store.astype(jnp.bfloat16), DP, split_axis=0, concat_...  14.4 us
    all_to_all x2, waiting for transfers between devices, sent_to_all(): return lax.all_to_all(copies, axis, split_axis=0, concat_axis=0, tiled=True)  10 us
  transfers between devices with their start and end apart: 8, of which 7 were waited for; matrix products, arithmetic and copies ran while one was open for 3% of the time, Pallas kernels for 0%

commit v1 on v0

--- a/solution.py
+++ b/solution.py
@@ -103,7 +103,7 @@
     preact = jnp.dot(normed, picture_entry_matrix, preferred_element_type=jnp.float32)
     hidden = gelu_tanh(preact).astype(jnp.bfloat16)
     partial_out = jnp.dot(hidden, picture_exit_matrix, preferred_element_type=jnp.float32)
-    image_out = image_float + lax.psum(partial_out, "mp")
+    image_out = image_float + jnp.sum(lax.all_gather(partial_out, "mp"), axis=0)
     inv_image = lax.rsqrt(jnp.sum(image_out * image_out, axis=-1, keepdims=True) + 1e-06)
     unit_image = (image_out * inv_image).astype(jnp.bfloat16)
     text_out = summed_on_arrival(

time: 419 us -> 529 us (1.26)
  waiting for transfers between devices: 299 us -> 404 us
    all_gather x0 -> x1, waiting for transfers between devices: none -> 111 us  [per_device(): image_out = image_float + jnp.sum(lax.all_gather(partial_out, 'mp'), axis=0)]
    psum x1 -> x0, waiting for transfers between devices: 33 us -> none  [per_device(): image_out = image_float + lax.psum(partial_out, 'mp')]
    all_gather x2, waiting for transfers between devices: 69.5 us -> 90.5 us  [stacked_from(): parts = lax.all_gather(parts, axes[k], axis=0, tiled=True)]
    all_to_all x2, waiting for transfers between devices: 23.6 us -> 29.2 us  [sum_at_owner(): lax.all_to_all(parts, axis, split_axis=0, concat_axis=0, tiled=True)]
  transfers between devices with their start and end apart: 8 -> 8, of which waited for: 7 -> 8; matrix products, arithmetic and copies ran while one was open for 3% -> 3% of each run, Pallas kernels for 0% -> 0%
where the time goes in v1:
time: 529 us; the launch traced here: 528 us
  waiting for transfers between devices  404 us (76%)
  blocking collectives  40 us (8%)
  starting transfers between devices  29.7 us (6%)
  matrix products  17.4 us (3%)
  between operations  15.2 us (3%)
  other arithmetic  12 us (2%)
  local copies, waits for them, and re-layouts  10 us (2%)
    all_to_all x1, waiting for transfers between devices, per_device(): lax.all_to_all(text_store.astype(jnp.bfloat16), DP, split_axis=0, concat_...  163 us
    all_gather x1, waiting for transfers between devices, per_device(): image_out = image_float + jnp.sum(lax.all_gather(partial_out, 'mp'), axis=0)  111 us
    all_gather x2, waiting for transfers between devices, stacked_from(): parts = lax.all_gather(parts, axes[k], axis=0, tiled=True)  90.5 us
    all_to_all x2, waiting for transfers between devices, sum_at_owner(): lax.all_to_all(parts, axis, split_axis=0, concat_axis=0, tiled=True)  29.2 us
    all_to_all x1, blocking collectives, sent_to_all(): return lax.all_to_all(copies, axis, split_axis=0, concat_axis=0, tiled=True)  18.7 us
    all_to_all x1, blocking collectives, summed_on_arrival(): parts = lax.all_to_all(cut_along(array, dim, peers), axis, 0, 0, tiled=True)  16.3 us
    all_to_all x1, starting transfers between devices, per_device(): lax.all_to_all(text_store.astype(jnp.bfloat16), DP, split_axis=0, concat_...  14.4 us
  transfers between devices with their start and end apart: 8, of which 8 were waited for; matrix products, arithmetic and copies ran while one was open for 3% of the time, Pallas kernels for 0%

profile of v1, /device:TPU:8, one launch (start us, length us, event | category | flops | bytes accessed | tf_op | source)
XLA Modules:
  0.0 528.2 jit_solution(9522843680773712987)
XLA Ops:
  7.2 1.4 convolution_convert_fusion.1
  8.7 16.3 %all_to_all.40 = bf16[8,24,1152]{2,1,0:T(8,128)(2,1)S(1)} all-to-all(bf16[8,24,1152]{2,1,0:T(8,128)(2,1)S(1)} %bitcast.52), channel_id=1, replica_groups=mesh['dp_0'=16,'dp_1'=2,'dp_2'=2,'mp'=8] {'mp'}, dimensions={0} | all-to-all | bytes 884736 | tf_op jit(solution)/shard_map/all_to_all | solution.py:18
  25.2 4.9 all_gather.17
  30.2 73.9 %all-gather.5.cloned.1.call-done = bf16[32,24,1152]{2,1,0:T(8,128)(2,1)} async-done(((bf16[2,24,1152]{2,1,0:T(8,128)(2,1)}), bf16[32,24,1152]{2,1,0:T(8,128)(2,1)}) %all-gather.5.cloned.1.call-update) | async-done | bytes 1769488 | tf_op jit(solution)/shard_map/all_gather | solution.py:31
  106.9 1.5 fusion.32
  109.7 16.6 %all-gather.7.cloned.1.call-done = bf16[64,24,1152]{2,1,0:T(8,128)(2,1)} async-done(((bf16[32,24,1152]{2,1,0:T(8,128)(2,1)}), bf16[64,24,1152]{2,1,0:T(8,128)(2,1)}) %all-gather.7.cloned.1.call-update) | async-done | bytes 3538960 | tf_op jit(solution)/shard_map/all_gather | solution.py:31
  126.4 4.2 copy.27
  130.5 111.3 %all-gather.9.cloned.1.call-done = f32[1536,1152]{1,0:T(8,128)} async-done(((f32[192,1152]{1,0:T(8,128)}), f32[1536,1152]{1,0:T(8,128)}) %all-gather.9.cloned.1.call-update) | async-done | bytes 7077904 | tf_op jit(solution)/shard_map/all_gather | solution.py:106
  241.8 3.5 reduce_sum.130
  245.5 1.3 fusion.7
  246.8 0.8 copy-done.1
  247.6 2.5 fusion.6
  250.1 1.9 fusion.74
  252.0 3.6 all-to-all-start.1
  255.7 13.6 %all-to-all-done.1 = f32[8,24,1152]{2,1,0:T(8,128)S(1)} async-done(((f32[8,24,1152]{2,1,0:T(8,128)}), f32[8,24,1152]{2,1,0:T(8,128)S(1)}, u32[]{:S(2)}, u32[]{:S(2)}) %all-to-all-start.1) | async-done | bytes 884768 | tf_op jit(solution)/shard_map/all_to_all | solution.py:44
  269.7 18.7 %all_to_all.41 = f32[8,24,1152]{2,1,0:T(8,128)S(1)} all-to-all(f32[8,24,1152]{2,1,0:T(8,128)S(1)} %broadcast_in_dim.36), channel_id=1, replica_groups=mesh['dp_0'=16,'dp_1'=2,'dp_2'=2,'mp'=8] {'mp'}, dimensions={0} | all-to-all | bytes 1769472 | tf_op jit(solution)/shard_map/all_to_all | solution.py:50
  288.4 3.7 fusion.28
  292.1 3.6 all-to-all-start.3
  295.8 15.6 %all-to-all-done.3 = f32[8,192,144]{1,2,0:T(8,128)S(1)} async-done(((f32[8,192,144]{1,2,0:T(8,128)}), f32[8,192,144]{1,2,0:T(8,128)S(1)}, u32[]{:S(2)}, u32[]{:S(2)}) %all-to-all-start.3) | async-done | bytes 884768 | tf_op jit(solution)/shard_map/all_to_all | solution.py:44
  312.1 1.0 copy.29
  313.2 1.2 multiply_reduce_fusion.2
  315.0 3.8 all-to-all-start.4
  318.9 4.7 convolution_convert_fusion
  323.6 2.9 all-to-all-done.4
  326.6 14.4 %all-to-all-start.5 = ((bf16[64,24,1152]{2,1,0:T(8,128)(2,1)}), bf16[64,24,1152]{2,1,0:T(8,128)(2,1)}, u32[]{:S(2)}, u32[]{:S(2)}) async-start(bf16[64,24,1152]{2,1,0:T(8,128)(2,1)} %bitcast.50), calls=%async_computation.5 | async-start | bytes 7077888 | tf_op jit(solution)/shard_map/all_to_all | solution.py:143
  341.0 162.7 %all-to-all-done.5 = bf16[64,24,1152]{2,1,0:T(8,128)(2,1)} async-done(((bf16[64,24,1152]{2,1,0:T(8,128)(2,1)}), bf16[64,24,1152]{2,1,0:T(8,128)(2,1)}, u32[]{:S(2)}, u32[]{:S(2)}) %all-to-all-start.5) | async-done | bytes 3538976 | tf_op jit(solution)/shard_map/all_to_all | solution.py:143
  503.7 2.5 convert_reduce_fusion
  506.5 0.8 broadcast_in_dim.40
  507.3 4.3 all-to-all-start.6
  511.6 1.2 multiply_add_fusion
  513.6 7.1 %all-to-all-done.6 = bf16[8,24,1152]{2,1,0:T(8,128)(2,1)S(1)} async-done(((bf16[8,24,1152]{2,1,0:T(8,128)(2,1)}), bf16[8,24,1152]{2,1,0:T(8,128)(2,1)S(1)}, u32[]{:S(2)}, u32[]{:S(2)}) %all-to-all-start.6) | async-done | bytes 442400 | tf_op jit(solution)/shard_map/all_to_all | solution.py:50
  520.7 1.0 fusion.75
  (50 shorter events, 6.4 us)
Async XLA Ops:
  7.2 99.7 %copy-start = (bf16[538,1152]{1,0:T(8,128)(2,1)S(1)}, bf16[538,1152]{1,0:T(8,128)(2,1)}, u32[]{:S(2)}) copy-start(bf16[538,1152]{1,0:T(8,128)(2,1)} %param.12) | copy-start | bytes 3718660
  7.2 96.9 %all-gather.5.cloned.1.call-start = ((), (), s32[]{:S(2)}) async-start(), calls=%async_computation.7 | async-start | bytes 1880064 | tf_op jit(solution)/shard_map/all_gather | solution.py:31
  25.0 79.2 %copy-start.2 = (bf16[192,1152]{1,0:T(8,128)(2,1)S(1)}, bf16[192,1152]{1,0:T(8,128)(2,1)}, u32[]{:S(2)}) copy-start(bf16[192,1152]{1,0:T(8,128)(2,1)} %param.8) | copy-start | bytes 1327108
  30.2 96.2 %all-gather.7.cloned.1.call-start = ((), (), s32[]{:S(2)}) async-start(), calls=%async_computation.8 | async-start | bytes 5308416 | tf_op jit(solution)/shard_map/all_gather | solution.py:31
  104.1 0.7 copy-start.7
  104.1 1.3 copy-start.8
  104.1 137.7 %all-gather.9.cloned.1.call-start = ((), (), s32[]{:S(2)}) async-start(), calls=%async_computation.9 | async-start | bytes 7962624 | tf_op jit(solution)/shard_map/all_gather | solution.py:106
  106.1 0.8 copy-start.5
  245.3 2.3 copy-start.1
  246.8 22.7 %copy-start.4 = (bf16[192,1152]{1,0:T(8,128)(2,1)}, bf16[192,1152]{1,0:T(8,128)(2,1)S(1)}, u32[]{:S(2)}) copy-start(bf16[192,1152]{1,0:T(8,128)(2,1)S(1)} %get-tuple-element.13) | copy-start | bytes 1327108
  252.0 17.3 %all-to-all-start.1 = ((f32[8,24,1152]{2,1,0:T(8,128)}), f32[8,24,1152]{2,1,0:T(8,128)S(1)}, u32[]{:S(2)}, u32[]{:S(2)}) async-start(f32[8,24,1152]{2,1,0:T(8,128)} %fusion.74), calls=%async_computation.1 | async-start | bytes 1769472 | tf_op jit(solution)/shard_map/all_to_all | solution.py:44
  269.6 18.8 %copy-start.6 = (f32[192,538]{1,0:T(8,128)S(1)}, f32[192,538]{1,0:T(8,128)}, u32[]{:S(2)}) copy-start(f32[192,538]{1,0:T(8,128)} %copy-done.5) | copy-start | bytes 1239556
  292.1 19.3 %all-to-all-start.3 = ((f32[8,192,144]{1,2,0:T(8,128)}), f32[8,192,144]{1,2,0:T(8,128)S(1)}, u32[]{:S(2)}, u32[]{:S(2)}) async-start(f32[8,192,144]{1,2,0:T(8,128)} %bitcast.55), calls=%async_computation.3 | async-start | bytes 2359296 | tf_op jit(solution)/shard_map/all_to_all | solution.py:44
  315.0 11.5 %all-to-all-start.4 = ((f32[8,1,384]{2,1,0:T(1,128)}), f32[8,1,384]{2,1,0:T(1,128)S(1)}, u32[]{:S(2)}, u32[]{:S(2)}) async-start(f32[8,1,384]{2,1,0:T(1,128)} %broadcast_in_dim.37), calls=%async_computation.4 | async-start | bytes 24576 | tf_op jit(solution)/shard_map/all_to_all | solution.py:50
  326.6 177.1 %all-to-all-start.5 = ((bf16[64,24,1152]{2,1,0:T(8,128)(2,1)}), bf16[64,24,1152]{2,1,0:T(8,128)(2,1)}, u32[]{:S(2)}, u32[]{:S(2)}) async-start(bf16[64,24,1152]{2,1,0:T(8,128)(2,1)} %bitcast.50), calls=%async_computation.5 | async-start | bytes 7077888 | tf_op jit(solution)/shard_map/all_to_all | solution.py:143
  506.5 14.2 %copy-start.3 = (bf16[144,1152]{1,0:T(8,128)(2,1)S(1)}, bf16[144,1152]{1,0:T(8,128)(2,1)}, u32[]{:S(2)}) copy-start(bf16[144,1152]{1,0:T(8,128)(2,1)} %param.13) | copy-start | bytes 995332
  507.3 13.4 %all-to-all-start.6 = ((bf16[8,24,1152]{2,1,0:T(8,128)(2,1)}), bf16[8,24,1152]{2,1,0:T(8,128)(2,1)S(1)}, u32[]{:S(2)}, u32[]{:S(2)}) async-start(bf16[8,24,1152]{2,1,0:T(8,128)(2,1)} %broadcast_in_dim.40), calls=%async_computation.6 | async-start | bytes 884736 | tf_op jit(solution)/shard_map/all_to_all | solution.py:50
Sparse Core Ops, SparseCore 0:
  30.3 73.7 all-gather.4
  106.2 20.1 all-gather.6
  129.6 112.2 all-gather.8
